TPU v7x, 32 devices: a whole 2x2x4 slice. The times are simulated.
32 devices in a mesh: head: 2 (over y), seq: 16 (over z, x, core).
Axes of the slice: x: 2, y: 2, z: 4, core: 2. Of those that a mesh axis runs over, the one named last changes fastest.
Arguments:
- queries: bfloat16 [2048, 4096], P(('seq', 'head')), may hold values from -20 to 20
- keys: bfloat16 [2048, 1024], P(('seq', 'head')), may hold values from -5 to 5
- values: bfloat16 [2048, 1024], P(('seq', 'head')), may hold values from -6 to 6
Outputs:
- attended: bfloat16 [2048, 4096], P(('seq', 'head'))
All inputs are finite; a program needn't handle non-finite values.
Results may differ from a plain program's by a relative error of at most 0.0041.
Values may be sent and summed in bfloat16 or wider, within the bound.
No kernel may reach another device: no remote copies, remote signals or barrier semaphores. Data moves between devices by JAX's collectives and lax.ppermute only.
A program may use at most 64 MiB of HBM per device.

v0:
```python
import math

import jax
import jax.numpy as jnp
from jax import lax
from jax.sharding import PartitionSpec as P

HEAD_DIM = 128


def update_state(state, query_half, query_pos, key_piece, value_piece, key_pos):
    largest, total, summed = state
    score = jnp.einsum("tkgd,pkd->tkgp", query_half, key_piece, preferred_element_type=jnp.float32)
    score = score / math.sqrt(query_half.shape[-1])
    allowed = (key_pos[None, :] <= query_pos[:, None])[:, None, None, :]
    score = jnp.where(allowed, score, jnp.float32(-1e30))
    new_largest = jnp.maximum(largest, jnp.max(score, axis=-1))
    weight = jnp.where(allowed, jnp.exp(score - new_largest[..., None]), jnp.float32(0.0))
    total = jnp.sum(weight, axis=-1)
    product = jnp.einsum(
        "tkgp,pkd->tkgd",
        weight.astype(jnp.bfloat16),
        value_piece,
        preferred_element_type=jnp.float32,
    )
    summed = product
    return (new_largest, total, summed)


def on_device(queries, keys, values):
    q_local, k_local, v_local = (
        lax.all_to_all(queries, "head", split_axis=1, concat_axis=0, tiled=True),
        lax.all_to_all(keys, "head", split_axis=1, concat_axis=0, tiled=True),
        lax.all_to_all(values, "head", split_axis=1, concat_axis=0, tiled=True),
    )
    tokens = q_local.shape[0]
    half = tokens // 2
    kv_local = k_local.shape[1] // HEAD_DIM
    group = q_local.shape[1] // k_local.shape[1]
    index = lax.axis_index("seq")
    offsets = jnp.arange(half, dtype=jnp.int32)
    later = q_local[half:]
    early_pos = index * tokens + offsets
    later_pos = index * tokens + half + offsets
    query_pos = jnp.stack([early_pos, later_pos])
    halves = jnp.stack([q_local[:half], later]).reshape(2, half, kv_local, group, HEAD_DIM)
    start_state = (
        jnp.full((2, half, kv_local, group), -1e30, jnp.float32),
        jnp.zeros((2, half, kv_local, group), jnp.float32),
        jnp.zeros((2, half, kv_local, group, HEAD_DIM), jnp.float32),
    )
    start = jnp.int32(0)
    key_piece = lax.all_gather(k_local, "seq", axis=0, tiled=True)
    value_piece = lax.all_gather(v_local, "seq", axis=0, tiled=True)
    rows = key_piece.shape[0]
    key_piece = key_piece.reshape(rows, kv_local, HEAD_DIM)
    value_piece = value_piece.reshape(rows, kv_local, HEAD_DIM)
    key_pos = jnp.arange(rows, dtype=jnp.int32)
    results = []
    for which in range(2):
        state = (start_state[0][which], start_state[1][which], start_state[2][which])
        needed = start <= query_pos[which, half - 1]

        def run(current, which=which):
            return update_state(
                current, halves[which], query_pos[which], key_piece, value_piece, key_pos
            )

        def keep(current):
            return current

        results.append(lax.cond(needed, run, keep, state))
    total = jnp.stack([results[0][1], results[1][1]])
    summed = jnp.stack([results[0][2], results[1][2]])
    result = (summed / total[..., None]).reshape(2, half, q_local.shape[1]).astype(jnp.bfloat16)
    later_out = result[1]
    combined = jnp.concatenate([result[0], later_out], axis=0)
    return lax.all_to_all(combined, "head", split_axis=0, concat_axis=1, tiled=True)


def solution(mesh):
    return jax.shard_map(
        on_device,
        mesh=mesh,
        in_specs=(P(("seq", "head"), None), P(("seq", "head"), None), P(("seq", "head"), None)),
        out_specs=P(("seq", "head"), None),
        check_vma=False,
    )
```

profile of v0, /device:TPU:0, one launch (start us, length us, event | category | flops | bytes accessed | tf_op | source)
XLA Modules:
  0.0 142.9 jit_solution(106555980706747682)
XLA Ops:
  6.5 0.0 all-gather.3.cloned.1.call-start
  6.5 0.9 copy.81
  7.5 8.6 %all_to_all.73 = bf16[64,2,512]{2,0,1:T(8,128)(2,1)} all-to-all(bf16[64,2,512]{2,0,1:T(8,128)(2,1)S(1)} %bitcast.111), channel_id=1, replica_groups=mesh['head'=2,'seq'=16] {'head'}, dimensions={1} | all-to-all | bytes 262144 | tf_op jit(solution)/shard_map/all_to_all | solution.py:33
  16.1 0.0 all-gather.3.cloned.1.call-update
  16.1 0.0 all-gather.5.cloned.1.call-start
  16.2 0.9 copy.80
  17.1 7.5 %all_to_all.74 = bf16[64,2,512]{2,0,1:T(8,128)(2,1)} all-to-all(bf16[64,2,512]{2,0,1:T(8,128)(2,1)S(1)} %bitcast.112), channel_id=1, replica_groups=mesh['head'=2,'seq'=16] {'head'}, dimensions={1} | all-to-all | bytes 262144 | tf_op jit(solution)/shard_map/all_to_all | solution.py:34
  24.6 0.0 all-gather.5.cloned.1.call-update
  24.6 1.9 %copy.79 = bf16[8,2,8,2048]{3,2,0,1:T(8,128)(2,1)} copy(bf16[8,2,8,2048]{3,2,1,0:T(8,128)(2,1)} %bitcast.108) | data formatting | bytes 1048576 | tf_op jit(solution)/shard_map/all_to_all | solution.py:32
  26.5 3.5 %all-to-all-start = ((bf16[64,2,2048]{2,0,1:T(8,128)(2,1)}), bf16[64,2,2048]{2,0,1:T(8,128)(2,1)S(1)}, u32[]{:S(2)}, u32[]{:S(2)}) async-start(bf16[64,2,2048]{2,0,1:T(8,128)(2,1)} %bitcast.98), calls=%async_computation | async-start | bytes 1048576 | tf_op jit(solution)/shard_map/all_to_all | solution.py:32
  30.0 0.6 slice.29
  31.4 0.6 slice.26
  32.6 4.0 %all-to-all-done = bf16[64,2,2048]{2,0,1:T(8,128)(2,1)S(1)} async-done(((bf16[64,2,2048]{2,0,1:T(8,128)(2,1)}), bf16[64,2,2048]{2,0,1:T(8,128)(2,1)S(1)}, u32[]{:S(2)}, u32[]{:S(2)}) %all-to-all-start) | async-done | bytes 524320 | tf_op jit(solution)/shard_map/all_to_all | solution.py:32
  36.6 0.2 stack.42
  36.8 0.2 stack.41
  37.0 0.1 constant_dynamic-update-slice_fusion.1
  37.1 0.1 constant_dynamic-update-slice_fusion
  37.2 21.2 %all-gather.3.cloned.1.call-done = bf16[2048,512]{1,0:T(8,128)(2,1)} async-done(((bf16[128,512]{1,0:T(8,128)(2,1)}), bf16[2048,512]{1,0:T(8,128)(2,1)}) %all-gather.3.cloned.1.call-update) | async-done | bytes 2097168 | tf_op jit(solution)/shard_map/all_gather | solution.py:53
  58.4 2.9 %copy.49 = bf16[2048,512]{0,1:T(8,128)(2,1)S(1)} copy(bf16[2048,512]{1,0:T(8,128)(2,1)} %all-gather.3.cloned.1.call-done) | data formatting | bytes 4194304 | tf_op jit(solution)/shard_map/all_gather | solution.py:53
  61.3 39.4 %all-gather.5.cloned.1.call-done = bf16[2048,512]{1,0:T(8,128)(2,1)} async-done(((bf16[128,512]{1,0:T(8,128)(2,1)}), bf16[2048,512]{1,0:T(8,128)(2,1)}) %all-gather.5.cloned.1.call-update) | async-done | bytes 2097168 | tf_op jit(solution)/shard_map/all_gather | solution.py:54
  100.7 4.0 %copy.51 = bf16[2048,512]{0,1:T(8,128)(2,1)} copy(bf16[2048,512]{1,0:T(8,128)(2,1)} %all-gather.5.cloned.1.call-done) | data formatting | bytes 4194304 | tf_op jit(solution)/shard_map/all_gather | solution.py:54
  104.7 8.9 %conditional.2 = (f32[1,64,4,4]{1,3,2,0:T(4,128)S(1)}, f32[1,64,2048]{2,1,0:T(8,128)S(1)}) conditional(s32[]{:T(128)} %bitcast.12, () %tuple.29, (s32[2048]{0:T(1024)S(1)}, s32[]{:T(128)}, s32[64]{0:T(128)S(1)}, bf16[2,64,4,4,128]{4,3,2,1,0:T(4,128)(2,1)S(1)}, bf16[2048,4,128]{0,2,1:T(8,128)(2,1)S(1)}, ...), branch_computations={%region_0.0_spmd, %region_1.4_spmd} | conditional | flops 1101134848 | bytes 42238768 | solution.py:72
  104.8 0.1 broadcast_compare_fusion
  104.9 0.1 copy.52
  105.0 0.0 copy-start
  105.1 1.7 %fusion = (f32[64,4,4]{0,2,1:T(4,128)S(1)}, f32[4,2048,64,4]{1,2,3,0:T(8,128)S(1)}) fusion(pred[64,2048]{1,0:T(8,128)(4,1)S(1)} %broadcast_compare_fusion, bf16[2,64,4,4,128]{4,1,3,2,0:T(8,128)(2,1)S(1)} %copy.52, bf16[2048,4,128]{0,2,1:T(8,128)(2,1)S(1)} %get-tuple-element.97), kind=kOutput, calls=%fused_computation.2 | convolution fusion | flops 543161344 | bytes 10883072 | tf_op jit(solution)/shard_map/cond/branch_1_fun/tkgd,pkd->tkgp/dot_general | solution.py:13
  106.7 0.0 copy-done
  106.8 1.9 %fusion.9 = f32[64,4,4,128]{3,0,2,1:T(8,128)S(1)} fusion(bf16[2048,4,128]{0,2,1:T(8,128)(2,1)S(1)} %copy-done, f32[4,2048,64,4]{1,2,3,0:T(8,128)S(1)} %get-tuple-element.106, f32[64,4,4]{0,2,1:T(4,128)S(1)} %broadcast_maximum_fusion, pred[64,2048]{1,0:T(8,128)(4,1)S(1)} %broadcast_compare_fusion), kind=kOutput, calls=%fused_computation.10 | convolution fusion | flops 547356672 | bytes 11145216 | tf_op jit(solution)/shard_map/cond/branch_1_fun/tkgp,pkd->tkgd/dot_general | solution.py:20
  108.7 2.5 %fusion.2 = f32[64,4,4]{0,2,1:T(4,128)S(1)} fusion(f32[4,2048,64,4]{1,2,3,0:T(8,128)S(1)} %get-tuple-element.106, f32[64,4,4]{0,2,1:T(4,128)S(1)} %broadcast_maximum_fusion, pred[64,2048]{1,0:T(8,128)(4,1)S(1)} %broadcast_compare_fusion), kind=kLoop, calls=%fused_computation.4 | loop fusion | flops 10484736 | bytes 8527872 | tf_op jit(solution)/shard_map/cond/branch_1_fun/reduce_sum | solution.py:19
  111.2 1.1 copy.45
  112.4 1.3 stack.31
  113.6 8.0 %conditional.3 = (f32[1,64,4,4]{1,3,2,0:T(4,128)S(1)}, f32[1,64,2048]{2,1,0:T(8,128)}) conditional(s32[]{:T(128)} %bitcast.20, () %tuple.31, (s32[2048]{0:T(1024)S(1)}, s32[]{:T(128)}, s32[64]{0:T(128)S(1)}, bf16[2,64,4,4,128]{4,3,2,1,0:T(4,128)(2,1)S(1)}, bf16[2048,4,128]{0,2,1:T(8,128)(2,1)S(1)}, /*index=5*/bf16[2048,4,128]{0,2,1:T(8,128)(2,1)}) %tuple.56), branch_computations={%region_4.5_spmd, %region_5.8_spmd} | conditional | flops 1101134848 | bytes 42238768 | solution.py:72
  113.8 0.1 broadcast_compare_fusion.1
  114.0 0.1 copy.55
  114.1 0.0 copy-start.1
  114.1 1.7 %fusion.17 = (f32[64,4,4]{0,2,1:T(4,128)S(1)}, f32[4,2048,64,4]{1,2,3,0:T(8,128)S(1)}) fusion(pred[64,2048]{1,0:T(8,128)(4,1)S(1)} %broadcast_compare_fusion.1, bf16[2,64,4,4,128]{4,1,3,2,0:T(8,128)(2,1)S(1)} %copy.55, bf16[2048,4,128]{0,2,1:T(8,128)(2,1)S(1)} %get-tuple-element.103), kind=kOutput, calls=%fused_computation.20 | convolution fusion | flops 543161344 | bytes 10883072 | tf_op jit(solution)/shard_map/cond/branch_1_fun/tkgd,pkd->tkgp/dot_general | solution.py:13
  115.8 0.0 copy-done.1
  115.8 1.9 %fusion.26 = f32[64,4,4,128]{3,0,2,1:T(8,128)S(1)} fusion(bf16[2048,4,128]{0,2,1:T(8,128)(2,1)S(1)} %copy-done.1, f32[4,2048,64,4]{1,2,3,0:T(8,128)S(1)} %get-tuple-element.108, f32[64,4,4]{0,2,1:T(4,128)S(1)} %broadcast_maximum_fusion.1, pred[64,2048]{1,0:T(8,128)(4,1)S(1)} %broadcast_compare_fusion.1), kind=kOutput, calls=%fused_computation.28 | convolution fusion | flops 547356672 | bytes 11145216 | tf_op jit(solution)/shard_map/cond/branch_1_fun/tkgp,pkd->tkgd/dot_general | solution.py:20
  117.8 2.5 %fusion.19 = f32[64,4,4]{0,2,1:T(4,128)S(1)} fusion(f32[4,2048,64,4]{1,2,3,0:T(8,128)S(1)} %get-tuple-element.108, f32[64,4,4]{0,2,1:T(4,128)S(1)} %broadcast_maximum_fusion.1, pred[64,2048]{1,0:T(8,128)(4,1)S(1)} %broadcast_compare_fusion.1), kind=kLoop, calls=%fused_computation.22 | loop fusion | flops 10484736 | bytes 8527872 | tf_op jit(solution)/shard_map/cond/branch_1_fun/reduce_sum | solution.py:19
  120.3 0.3 copy.46
  120.7 1.0 stack.35
  121.7 0.2 copy.58
  121.9 0.6 div.21
  122.5 0.4 div.22
  122.9 1.2 fusion.34
  124.2 11.1 %all_to_all.75 = bf16[2,64,2048]{2,1,0:T(8,128)(2,1)S(1)} all-to-all(bf16[2,64,2048]{2,1,0:T(8,128)(2,1)S(1)} %bitcast.106), channel_id=1, replica_groups=mesh['head'=2,'seq'=16] {'head'}, dimensions={0} | all-to-all | bytes 1048576 | tf_op jit(solution)/shard_map/all_to_all | solution.py:78
  135.2 0.8 copy.75
  (14 shorter events, 0.2 us)
Async XLA Ops:
  6.5 51.8 %all-gather.3.cloned.1.call-start = ((), (), s32[]{:S(2)}) async-start(), calls=%async_computation.4 | async-start | bytes 2228224 | tf_op jit(solution)/shard_map/all_gather | solution.py:53
  16.1 84.6 %all-gather.5.cloned.1.call-start = ((), (), s32[]{:S(2)}) async-start(), calls=%async_computation.5 | async-start | bytes 2228224 | tf_op jit(solution)/shard_map/all_gather | solution.py:54
  26.5 10.1 %all-to-all-start = ((bf16[64,2,2048]{2,0,1:T(8,128)(2,1)}), bf16[64,2,2048]{2,0,1:T(8,128)(2,1)S(1)}, u32[]{:S(2)}, u32[]{:S(2)}) async-start(bf16[64,2,2048]{2,0,1:T(8,128)(2,1)} %bitcast.98), calls=%async_computation | async-start | bytes 1048576 | tf_op jit(solution)/shard_map/all_to_all | solution.py:32
  105.0 1.7 %copy-start = (bf16[2048,4,128]{0,2,1:T(8,128)(2,1)S(1)}, bf16[2048,4,128]{0,2,1:T(8,128)(2,1)}, u32[]{:S(2)}) copy-start(bf16[2048,4,128]{0,2,1:T(8,128)(2,1)} %get-tuple-element.98) | copy-start | bytes 6291460 | tf_op jit(solution)/shard_map/cond
  114.1 1.7 %copy-start.1 = (bf16[2048,4,128]{0,2,1:T(8,128)(2,1)S(1)}, bf16[2048,4,128]{0,2,1:T(8,128)(2,1)}, u32[]{:S(2)}) copy-start(bf16[2048,4,128]{0,2,1:T(8,128)(2,1)} %get-tuple-element.104) | copy-start | bytes 6291460 | tf_op jit(solution)/shard_map/cond
Sparse Core Ops, SparseCore 0:
  16.2 42.0 all-gather.2
  60.5 40.1 all-gather.4
where the time goes:
time: 144 us; the launch traced here: 143 us
  waiting for transfers between devices  64.6 us (45%)
  blocking collectives  27.2 us (19%)
  local copies, waits for them, and re-layouts  18.5 us (13%)
  between operations  14.8 us (10%)
  matrix products  7.21 us (5%)
  other arithmetic  6.63 us (5%)
  starting transfers between devices  3.53 us (2%)
    all_gather x1, waiting for transfers between devices, on_device(): value_piece = lax.all_gather(v_local, 'seq', axis=0, tiled=True)  39.4 us
    all_gather x1, waiting for transfers between devices, on_device(): key_piece = lax.all_gather(k_local, 'seq', axis=0, tiled=True)  21.2 us
    all_to_all x1, blocking collectives, on_device(): lax.all_to_all(combined, 'head', split_axis=0, concat_axis=1, tiled=True)  11.1 us
    all_to_all x1, blocking collectives, on_device(): lax.all_to_all(keys, 'head', split_axis=1, concat_axis=0, tiled=True)  8.64 us
    all_to_all x1, blocking collectives, on_device(): lax.all_to_all(values, 'head', split_axis=1, concat_axis=0, tiled=True)  7.52 us
    reduce_sum x2, other arithmetic, update_state(): total = jnp.sum(weight, axis=-1)  5.08 us
    all_to_all x1, waiting for transfers between devices, on_device(): lax.all_to_all(queries, 'head', split_axis=1, concat_axis=0, tiled=True)  3.99 us
    all_gather x1, local copies, waits for them, and re-layouts, on_device(): value_piece = lax.all_gather(v_local, 'seq', axis=0, tiled=True)  3.95 us
  transfers between devices with their start and end apart: 3, of which 3 were waited for; matrix products, arithmetic and copies ran while one was open for 5% of the time, Pallas kernels for 0%

commit v1 on v0

v1 whole, which is shorter than its diff:
```python
import functools
import math

import jax
import jax.numpy as jnp
from jax import lax
from jax.experimental import pallas as pl
from jax.experimental.pallas import tpu as pltpu
from jax.sharding import Mesh, PartitionSpec as P

HEAD_DIM = 128
SCALE = math.log2(math.e) / math.sqrt(HEAD_DIM)
DIMS_NT = (((1,), (1,)), ((), ()))


def attend_kernel(plane_ref, q_ref, kv_ref, out_ref, *, block):
    plane = plane_ref[0]
    tile = q_ref.shape[0]
    row_block = pl.program_id(0)
    q = q_ref[...]

    def step(start, width, state, masked):
        largest, total, summed = state
        k = kv_ref[pl.ds(start, width), :HEAD_DIM]
        v = kv_ref[pl.ds(start, width), HEAD_DIM:]
        score = lax.dot_general(q, k, DIMS_NT, preferred_element_type=jnp.float32)
        if masked:
            row = lax.broadcasted_iota(jnp.int32, score.shape, 0)
            col = lax.broadcasted_iota(jnp.int32, score.shape, 1)
            score = jnp.where(col <= row + row_block * tile, score, jnp.float32(-1e30))
        new_largest = jnp.maximum(largest, jnp.max(score, axis=1, keepdims=True))
        weight = jnp.exp2((score - new_largest) * SCALE)
        fade = jnp.exp2((largest - new_largest) * SCALE)
        total = total * fade + jnp.sum(weight, axis=1, keepdims=True)
        summed = summed * fade + jnp.dot(
            weight.astype(jnp.bfloat16), v, preferred_element_type=jnp.float32
        )
        return new_largest, total, summed

    state = (
        jnp.full((tile, 1), -1e30, jnp.float32),
        jnp.zeros((tile, 1), jnp.float32),
        jnp.zeros((tile, HEAD_DIM), jnp.float32),
    )
    state = step(pl.multiple_of(plane * block, block), block, state, True)
    state = lax.fori_loop(
        0, plane, lambda i, s: step(pl.multiple_of(i * block, block), block, s, False), state
    )
    out_ref[...] = (state[2] / state[1]).astype(jnp.bfloat16)


def attend(plane, queries, kv):
    rows, width = queries.shape
    keys = kv.shape[0]
    block = rows
    tile = min(rows, 256)
    return pl.pallas_call(
        functools.partial(attend_kernel, block=block),
        grid=(rows // tile, width // HEAD_DIM),
        in_specs=[
            pl.BlockSpec(memory_space=pltpu.SMEM),
            pl.BlockSpec((tile, HEAD_DIM), lambda r, h: (r, h)),
            pl.BlockSpec((keys, 2 * HEAD_DIM), lambda r, h: (0, 0)),
        ],
        out_specs=pl.BlockSpec((tile, HEAD_DIM), lambda r, h: (r, h)),
        out_shape=jax.ShapeDtypeStruct((rows, width), jnp.bfloat16),
        name="attend",
    )(plane, queries, kv)


def on_device(queries, keys, values, *, outer, groups):
    rows = queries.shape[0]
    plane = lax.axis_index("outer")
    paired = jnp.concatenate(
        [keys.reshape(rows, groups, -1), values.reshape(rows, groups, -1)], axis=2
    ).reshape(rows, -1)
    axes = ("inner", "head")
    kv_own = lax.all_to_all(paired, axes, split_axis=1, concat_axis=0, tiled=True)
    q_own = lax.all_to_all(queries, axes, split_axis=1, concat_axis=0, tiled=True)
    if outer <= 8:
        block = kv_own.shape[0]
        kv = jnp.zeros((outer * block, kv_own.shape[1]), kv_own.dtype)
        kv = lax.dynamic_update_slice(kv, kv_own, (plane * block, 0))
        for shift in range(1, outer):
            moved = lax.ppermute(kv_own, "outer", [(i, i + shift) for i in range(outer - shift)])
            source = jnp.where(plane >= shift, plane - shift, plane - shift + outer)
            kv = lax.dynamic_update_slice(kv, moved, (source * block, 0))
    else:
        kv = lax.all_gather(kv_own, "outer", axis=0, tiled=True)
    out = attend(plane.reshape(1).astype(jnp.int32), q_own, kv)
    return lax.all_to_all(out, axes, split_axis=0, concat_axis=1, tiled=True)


def solution(mesh):
    def run(queries, keys, values):
        head, seq = mesh.shape["head"], mesh.shape["seq"]
        inner = math.gcd(seq, max(1, keys.shape[1] // HEAD_DIM // head))
        outer = seq // inner
        split = Mesh(mesh.devices.reshape(head, outer, inner), ("head", "outer", "inner"))
        spec = P(("outer", "inner", "head"), None)
        return jax.shard_map(
            functools.partial(on_device, outer=outer, groups=head * inner),
            mesh=split,
            in_specs=(spec, spec, spec),
            out_specs=spec,
            check_vma=False,
        )(queries, keys, values)

    return run
```

time: 144 us -> 72.4 us (0.50)
  the two profiles are of different devices: /device:TPU:0 before, /device:TPU:25 now
where the time goes in v1:
time: 72.4 us; the launch traced here: 71.7 us
  blocking collectives  23.3 us (32%)
  Pallas kernels  18.1 us (25%)
  waiting for transfers between devices  17.9 us (25%)
  starting transfers between devices  7.4 us (10%)
  local copies, waits for them, and re-layouts  4.82 us (7%)
    pallas_call x1, Pallas kernels, attend(): pl.pallas_call(functools.partial(attend_kernel, block=block), grid=(rows...  18.1 us
    ppermute x3, waiting for transfers between devices, on_device(): lax.ppermute(kv_own, 'outer', [(i, i + shift) for i in range(outer - shif...  17.9 us
    all_to_all x1, blocking collectives, on_device(): return lax.all_to_all(out, axes, split_axis=0, concat_axis=1, tiled=True)  13.1 us
    all_to_all x1, blocking collectives, on_device(): lax.all_to_all(paired, axes, split_axis=1, concat_axis=0, tiled=True)  10.2 us
    ppermute x3, starting transfers between devices, on_device(): lax.ppermute(kv_own, 'outer', [(i, i + shift) for i in range(outer - shif...  3.85 us
    all_to_all x1, starting transfers between devices, on_device(): lax.all_to_all(queries, axes, split_axis=1, concat_axis=0, tiled=True)  3.54 us
    unnamed x8, local copies, waits for them, and re-layouts  2.02 us
  transfers between devices with their start and end apart: 4, of which 2 were waited for; matrix products, arithmetic and copies ran while one was open for 1% of the time, Pallas kernels for 0%

profile of v1, /device:TPU:25, one launch (start us, length us, event | category | flops | bytes accessed | tf_op | source)
XLA Modules:
  0.0 71.7 jit_solution(828725450482133595)
XLA Ops:
  0.0 0.0 copy-start
  0.0 0.9 %copy-done = bf16[64,1024]{1,0:T(8,128)(2,1)S(1)} copy-done((bf16[64,1024]{1,0:T(8,128)(2,1)S(1)}, bf16[64,1024]{1,0:T(8,128)(2,1)}, u32[]{:S(2)}) %copy-start) | copy-done | bytes 131096
  0.9 1.0 %copy_bitcast_fusion.1 = (bf16[64,8,128]{2,0,1:T(8,128)(2,1)S(1)}, bf16[64,8,128]{2,0,1:T(8,128)(2,1)S(1)}) fusion(bf16[64,1024]{1,0:T(8,128)(2,1)S(1)} %copy-done, bf16[64,1024]{1,0:T(8,128)(2,1)} %param.5), kind=kLoop, calls=%fused_computation.2 | loop fusion | bytes 524288 | tf_op jit(solution)/shard_map/reshape | solution.py:75
  1.9 0.0 copy-start.3
  1.9 10.2 %all_to_all.54 = bf16[64,8,256]{2,0,1:T(8,128)(2,1)S(1)} all-to-all(bf16[64,8,256]{2,0,1:T(8,128)(2,1)S(1)} %pad_maximum_fusion), channel_id=1, replica_groups=mesh['head'=2,'outer'=4,'inner'=4] {'inner','head'}, dimensions={1} | all-to-all | bytes 524288 | tf_op jit(solution)/shard_map/all_to_all | solution.py:78
  12.1 1.3 %collective-permute-start = (bf16[512,256]{1,0:T(8,128)(2,1)S(1)}, bf16[512,256]{1,0:T(8,128)(2,1)S(1)}, u32[]{:S(2)}, u32[]{:S(2)}) collective-permute-start(bf16[512,256]{1,0:T(8,128)(2,1)S(1)} %bitcast.28), channel_id=1, source_target_pairs={{0,4},{4,8},{8,12},{1,5},{5,9},{9,13},{2,6},{6,10},{10,14},{3,7},{... | collective-permute-start | bytes 786440 | tf_op jit(solution)/shard_map/ppermute | solution.py:85
  13.4 1.3 %collective-permute-start.1 = (bf16[512,256]{1,0:T(8,128)(2,1)S(1)}, bf16[512,256]{1,0:T(8,128)(2,1)S(1)}, u32[]{:S(2)}, u32[]{:S(2)}) collective-permute-start(bf16[512,256]{1,0:T(8,128)(2,1)S(1)} %bitcast.29), channel_id=1, source_target_pairs={{0,8},{4,12},{1,9},{5,13},{2,10},{6,14},{3,11},{7,15},{16,24},{20,... | collective-permute-start | bytes 786440 | tf_op jit(solution)/shard_map/ppermute | solution.py:85
  14.7 0.0 copy-done.3
  14.7 0.8 %copy.15 = bf16[8,8,8,512]{3,2,0,1:T(8,128)(2,1)} copy(bf16[8,8,8,512]{3,2,1,0:T(8,128)(2,1)S(1)} %bitcast.32) | data formatting | bytes 1048576 | tf_op jit(solution)/shard_map/all_to_all | solution.py:79
  15.6 3.5 %all-to-all-start = ((bf16[64,8,512]{2,0,1:T(8,128)(2,1)}), bf16[64,8,512]{2,0,1:T(8,128)(2,1)S(1)}, u32[]{:S(2)}, u32[]{:S(2)}) async-start(bf16[64,8,512]{2,0,1:T(8,128)(2,1)} %bitcast.24), calls=%async_computation | async-start | bytes 1048576 | tf_op jit(solution)/shard_map/all_to_all | solution.py:79
  19.1 1.3 %collective-permute-start.2 = (bf16[512,256]{1,0:T(8,128)(2,1)S(1)}, bf16[512,256]{1,0:T(8,128)(2,1)S(1)}, u32[]{:S(2)}, u32[]{:S(2)}) collective-permute-start(bf16[512,256]{1,0:T(8,128)(2,1)S(1)} %bitcast.30), channel_id=1, source_target_pairs={{0,12},{1,13},{2,14},{3,15},{16,28},{17,29},{18,30},{19,31}} | collective-permute-start | bytes 786440 | tf_op jit(solution)/shard_map/ppermute | solution.py:85
  20.4 0.1 broadcast_in_dim.3
  20.5 1.2 %collective-permute-done = bf16[512,256]{1,0:T(8,128)(2,1)S(1)} collective-permute-done((bf16[512,256]{1,0:T(8,128)(2,1)S(1)}, bf16[512,256]{1,0:T(8,128)(2,1)S(1)}, u32[]{:S(2)}, u32[]{:S(2)}) %collective-permute-start) | collective-permute-done | bytes 262176 | tf_op jit(solution)/shard_map/ppermute | solution.py:85
  21.7 16.7 %collective-permute-done.1 = bf16[512,256]{1,0:T(8,128)(2,1)S(1)} collective-permute-done((bf16[512,256]{1,0:T(8,128)(2,1)S(1)}, bf16[512,256]{1,0:T(8,128)(2,1)S(1)}, u32[]{:S(2)}, u32[]{:S(2)}) %collective-permute-start.1) | collective-permute-done | bytes 262176 | tf_op jit(solution)/shard_map/ppermute | solution.py:85
  38.5 0.0 collective-permute-done.2
  38.5 0.0 copy-start.1
  38.5 0.0 all-to-all-done
  38.5 0.0 copy-start.2
  38.6 0.9 %copy-done.1 = bf16[2048,256]{1,0:T(8,128)(2,1)} copy-done((bf16[2048,256]{1,0:T(8,128)(2,1)}, bf16[2048,256]{1,0:T(8,128)(2,1)S(1)}, u32[]{:S(2)}) %copy-start.1) | copy-done | bytes 1048600
  39.5 0.2 copy-done.2
  39.7 18.1 %attend.1 = bf16[512,512]{1,0:T(8,128)(2,1)} custom-call(s32[1]{0:T(128)} %bitcast.plane_ref, bf16[512,512]{1,0:T(8,128)(2,1)} %bitcast.25, bf16[2048,256]{1,0:T(8,128)(2,1)} %copy-done.1), custom_call_target="tpu_custom_call" | custom-call | tf_op jit(solution)/shard_map/attend/pallas_call | solution.py:57
  57.8 13.1 %all_to_all.55 = bf16[8,64,512]{2,1,0:T(8,128)(2,1)S(1)} all-to-all(bf16[8,64,512]{2,1,0:T(8,128)(2,1)} %bitcast.26), channel_id=1, replica_groups=mesh['head'=2,'outer'=4,'inner'=4] {'inner','head'}, dimensions={0} | all-to-all | bytes 1048576 | tf_op jit(solution)/shard_map/all_to_all | solution.py:91
  70.9 0.8 %copy.11 = bf16[8,8,8,512]{3,2,0,1:T(8,128)(2,1)} copy(bf16[8,8,8,512]{3,2,1,0:T(8,128)(2,1)S(1)} %bitcast.27) | data formatting | bytes 1048576 | tf_op jit(solution)/shard_map/all_to_all | solution.py:91
  (5 shorter events, 0.1 us)
Async XLA Ops:
  0.0 0.9 %copy-start = (bf16[64,1024]{1,0:T(8,128)(2,1)S(1)}, bf16[64,1024]{1,0:T(8,128)(2,1)}, u32[]{:S(2)}) copy-start(bf16[64,1024]{1,0:T(8,128)(2,1)} %param.4) | copy-start | bytes 393220
  1.9 12.8 %copy-start.3 = (bf16[64,4096]{1,0:T(8,128)(2,1)S(1)}, bf16[64,4096]{1,0:T(8,128)(2,1)}, u32[]{:S(2)}) copy-start(bf16[64,4096]{1,0:T(8,128)(2,1)} %param.3) | copy-start | bytes 1572868
  12.1 9.6 %collective-permute-start = (bf16[512,256]{1,0:T(8,128)(2,1)S(1)}, bf16[512,256]{1,0:T(8,128)(2,1)S(1)}, u32[]{:S(2)}, u32[]{:S(2)}) collective-permute-start(bf16[512,256]{1,0:T(8,128)(2,1)S(1)} %bitcast.28), channel_id=1, source_target_pairs={{0,4},{4,8},{8,12},{1,5},{5,9},{9,13},{2,6},{6,10},{10,14},{3,7},{... | collective-permute-start | bytes 786440 | tf_op jit(solution)/shard_map/ppermute | solution.py:85
  13.4 25.1 %collective-permute-start.1 = (bf16[512,256]{1,0:T(8,128)(2,1)S(1)}, bf16[512,256]{1,0:T(8,128)(2,1)S(1)}, u32[]{:S(2)}, u32[]{:S(2)}) collective-permute-start(bf16[512,256]{1,0:T(8,128)(2,1)S(1)} %bitcast.29), channel_id=1, source_target_pairs={{0,8},{4,12},{1,9},{5,13},{2,10},{6,14},{3,11},{7,15},{16,24},{20,... | collective-permute-start | bytes 786440 | tf_op jit(solution)/shard_map/ppermute | solution.py:85
  15.6 23.0 %all-to-all-start = ((bf16[64,8,512]{2,0,1:T(8,128)(2,1)}), bf16[64,8,512]{2,0,1:T(8,128)(2,1)S(1)}, u32[]{:S(2)}, u32[]{:S(2)}) async-start(bf16[64,8,512]{2,0,1:T(8,128)(2,1)} %bitcast.24), calls=%async_computation | async-start | bytes 1048576 | tf_op jit(solution)/shard_map/all_to_all | solution.py:79
  19.1 19.4 %collective-permute-start.2 = (bf16[512,256]{1,0:T(8,128)(2,1)S(1)}, bf16[512,256]{1,0:T(8,128)(2,1)S(1)}, u32[]{:S(2)}, u32[]{:S(2)}) collective-permute-start(bf16[512,256]{1,0:T(8,128)(2,1)S(1)} %bitcast.30), channel_id=1, source_target_pairs={{0,12},{1,13},{2,14},{3,15},{16,28},{17,29},{18,30},{19,31}} | collective-permute-start | bytes 786440 | tf_op jit(solution)/shard_map/ppermute | solution.py:85
  38.5 1.0 %copy-start.1 = (bf16[2048,256]{1,0:T(8,128)(2,1)}, bf16[2048,256]{1,0:T(8,128)(2,1)S(1)}, u32[]{:S(2)}) copy-start(bf16[2048,256]{1,0:T(8,128)(2,1)S(1)} %constant_dynamic-update-slice_fusion.kv_ref) | copy-start | bytes 3145732
  38.5 1.1 %copy-start.2 = (bf16[64,8,512]{2,0,1:T(8,128)(2,1)}, bf16[64,8,512]{2,0,1:T(8,128)(2,1)S(1)}, u32[]{:S(2)}) copy-start(bf16[64,8,512]{2,0,1:T(8,128)(2,1)S(1)} %all-to-all-done) | copy-start | bytes 1572868

commit v2 on v1

v2 whole, which is shorter than its diff:
```python
import functools
import math

import jax
import jax.numpy as jnp
from jax import lax
from jax.experimental import pallas as pl
from jax.experimental.pallas import tpu as pltpu
from jax.sharding import Mesh, PartitionSpec as P

HEAD_DIM = 128
SCALE = math.log2(math.e) / math.sqrt(HEAD_DIM)
DIMS_NT = (((1,), (1,)), ((), ()))
VMEM_LIMIT = 48 * 1024 * 1024


def scores(q, k):
    return lax.dot_general(q, k, DIMS_NT, preferred_element_type=jnp.float32)


def weigh(score, largest):
    weight = jnp.exp2((score - largest) * SCALE)
    return jnp.sum(weight, axis=1, keepdims=True), weight.astype(jnp.bfloat16)


def stack_heads(ref, start, rows):
    group = ref.shape[1] // HEAD_DIM
    return jnp.concatenate(
        [ref[pl.ds(start, rows), h * HEAD_DIM : (h + 1) * HEAD_DIM] for h in range(group)], axis=0
    )


def pack_state(largest, total, rows):
    lane = lax.broadcasted_iota(jnp.int32, (rows, HEAD_DIM), 1)
    return jnp.where(lane < HEAD_DIM // 2, largest, total)


def own_kernel(core_ref, q_ref, own_ref, other_ref, summed_ref, state_ref, *, run):
    group = q_ref.shape[1] // HEAD_DIM
    tall = group * run
    row = lax.broadcasted_iota(jnp.int32, (tall, run), 0) % run
    col = lax.broadcasted_iota(jnp.int32, (tall, run), 1)
    low = jnp.float32(-1e30)
    see_other = lax.broadcast(core_ref[0], (tall, run)) > 0
    for i in range(q_ref.shape[0] // run):
        q = stack_heads(q_ref, i * run, run)
        own = scores(q, own_ref[: (i + 1) * run, :HEAD_DIM])
        other = scores(q, other_ref[: (i + 1) * run, :HEAD_DIM])
        own_edge = jnp.where(col <= row, own[:, i * run :], low)
        other_edge = jnp.where(see_other, other[:, i * run :], low)
        if i:
            own_edge = jnp.concatenate([own[:, : i * run], own_edge], axis=1)
            other_edge = jnp.concatenate([other[:, : i * run], other_edge], axis=1)
        largest = jnp.maximum(
            jnp.max(own_edge, axis=1, keepdims=True), jnp.max(other_edge, axis=1, keepdims=True)
        )
        own_total, own_weight = weigh(own_edge, largest)
        other_total, other_weight = weigh(other_edge, largest)
        summed_ref[i * tall : (i + 1) * tall, :] = jnp.dot(
            own_weight, own_ref[: (i + 1) * run, HEAD_DIM:], preferred_element_type=jnp.float32
        ) + jnp.dot(
            other_weight, other_ref[: (i + 1) * run, HEAD_DIM:], preferred_element_type=jnp.float32
        )
        state_ref[i * tall : (i + 1) * tall, :] = pack_state(
            largest, own_total + other_total, tall
        )


def earlier_kernel(count_ref, q_ref, kv_ref, summed_in, state_in, *outs, run, last):
    group = q_ref.shape[1] // HEAD_DIM
    tall = group * run
    runs = q_ref.shape[0] // run
    half = HEAD_DIM // 2
    count = count_ref[0]

    def finish(i, summed, largest, total):
        if last:
            result = (summed / total).astype(jnp.bfloat16)
            for h in range(group):
                outs[0][pl.ds(i * run, run), h * HEAD_DIM : (h + 1) * HEAD_DIM] = result[
                    h * run : (h + 1) * run
                ]
        else:
            outs[0][pl.ds(i * tall, tall), :] = summed
            outs[1][pl.ds(i * tall, tall), :] = pack_state(largest, total, tall)

    @pl.when(count == 0)
    def _():
        for i in range(runs):
            state = state_in[i * tall : (i + 1) * tall, :]
            finish(i, summed_in[i * tall : (i + 1) * tall, :], state[:, :1], state[:, half : half + 1])

    @pl.when(count > 0)
    def _():
        for i in range(runs):
            q = stack_heads(q_ref, i * run, run)
            packed = state_in[i * tall : (i + 1) * tall, :]

            def step(block, carry, q=q):
                summed, largest, total = carry
                score = scores(q, kv_ref[block, :, :HEAD_DIM])
                new_largest = jnp.maximum(largest, jnp.max(score, axis=1, keepdims=True))
                fade = jnp.exp2((largest - new_largest) * SCALE)
                added, weight = weigh(score, new_largest)
                summed = summed * fade + jnp.dot(
                    weight, kv_ref[block, :, HEAD_DIM:], preferred_element_type=jnp.float32
                )
                return summed, new_largest, total * fade + added

            carry = (
                summed_in[i * tall : (i + 1) * tall, :],
                packed[:, :1],
                packed[:, half : half + 1],
            )
            if kv_ref.shape[0] == 1:
                carry = step(0, carry)
            else:
                carry = lax.fori_loop(0, count, step, carry)
            finish(i, *carry)


def attend_own(core, queries, own, other, run):
    rows, width = queries.shape
    tall = rows * (width // HEAD_DIM)
    whole = pl.BlockSpec(memory_space=pltpu.VMEM)
    shape = jax.ShapeDtypeStruct((tall, HEAD_DIM), jnp.float32)
    work = tall * rows
    return pl.pallas_call(
        functools.partial(own_kernel, run=run),
        in_specs=[pl.BlockSpec(memory_space=pltpu.SMEM), whole, whole, whole],
        out_specs=(whole, whole),
        out_shape=(shape, shape),
        compiler_params=pltpu.CompilerParams(vmem_limit_bytes=VMEM_LIMIT),
        cost_estimate=pl.CostEstimate(
            flops=8 * work * HEAD_DIM, transcendentals=2 * work, bytes_accessed=4 * tall * HEAD_DIM
        ),
        name="attend_own",
    )(core, queries, own, other)


def attend_earlier(count, queries, kv, summed, state, run, last):
    rows, width = queries.shape
    tall = rows * (width // HEAD_DIM)
    whole = pl.BlockSpec(memory_space=pltpu.VMEM)
    if last:
        shape = jax.ShapeDtypeStruct((rows, width), jnp.bfloat16)
    else:
        shape = (jax.ShapeDtypeStruct((tall, HEAD_DIM), jnp.float32),) * 2
    work = tall * kv.shape[0] * kv.shape[1]
    out = pl.pallas_call(
        functools.partial(earlier_kernel, run=run, last=last),
        in_specs=[pl.BlockSpec(memory_space=pltpu.SMEM), whole, whole, whole, whole],
        out_specs=whole if last else (whole, whole),
        out_shape=shape,
        compiler_params=pltpu.CompilerParams(vmem_limit_bytes=VMEM_LIMIT),
        cost_estimate=pl.CostEstimate(
            flops=4 * work * HEAD_DIM, transcendentals=work, bytes_accessed=4 * tall * HEAD_DIM
        ),
        name="attend_last" if last else "attend_earlier",
    )(count, queries, kv, summed, state)
    return out


def on_device(queries, keys, values, *, outer, groups, run):
    rows = queries.shape[0]
    scalar = lambda name: lax.axis_index(name).reshape(1).astype(jnp.int32)
    core, place = scalar("core"), scalar("outer")
    paired = jnp.concatenate(
        [keys.reshape(rows, groups, -1), values.reshape(rows, groups, -1)], axis=2
    ).reshape(rows, -1)
    axes = ("inner", "head")
    swap = [(0, 1), (1, 0)]
    own = lax.all_to_all(paired, axes, split_axis=1, concat_axis=0, tiled=True)
    q_own = lax.all_to_all(queries, axes, split_axis=1, concat_axis=0, tiled=True)
    if outer == 2:
        far = lax.ppermute(own, "outer", [(0, 1)])
        other = lax.ppermute(own, "core", swap)
        summed, state = attend_own(core, q_own, own, other, run)
        far, summed, state = lax.optimization_barrier((far, summed, state))
        far_other = lax.ppermute(far, "core", swap)
        summed, state = attend_earlier(place, q_own, far[None], summed, state, run, False)
        out = attend_earlier(place, q_own, far_other[None], summed, state, run, True)
    else:
        other = lax.ppermute(own, "core", swap)
        summed, state = attend_own(core, q_own, own, other, run)
        everything = lax.all_gather(own, ("outer", "core"), axis=0)
        out = attend_earlier(2 * place, q_own, everything, summed, state, run, True)
    return lax.all_to_all(out, axes, split_axis=0, concat_axis=1, tiled=True)


def solution(mesh):
    def run(queries, keys, values):
        head, seq = mesh.shape["head"], mesh.shape["seq"]
        inner = math.gcd(seq // 2, max(1, keys.shape[1] // HEAD_DIM // head))
        outer = seq // (2 * inner)
        split = Mesh(
            mesh.devices.reshape(head, outer, inner, 2), ("head", "outer", "inner", "core")
        )
        spec = P(("outer", "inner", "core", "head"), None)
        return jax.shard_map(
            functools.partial(
                on_device,
                outer=outer,
                groups=head * inner,
                run=queries.shape[0] // (seq * head) * head,
            ),
            mesh=split,
            in_specs=(spec, spec, spec),
            out_specs=spec,
            check_vma=False,
        )(queries, keys, values)

    return run
```

time: 72.4 us -> 63.8 us (0.88)
  the two profiles are of different devices: /device:TPU:25 before, /device:TPU:16 now
where the time goes in v2:
time: 63.8 us; the launch traced here: 63.4 us
  blocking collectives  20.3 us (32%)
  Pallas kernels  15.5 us (24%)
  waiting for transfers between devices  13.6 us (21%)
  starting transfers between devices  9.6 us (15%)
  local copies, waits for them, and re-layouts  3.55 us (6%)
  other arithmetic  0.74 us (1%)
    all_to_all x1, blocking collectives, on_device(): return lax.all_to_all(out, axes, split_axis=0, concat_axis=1, tiled=True)  20.3 us
    pallas_call x2, Pallas kernels, attend_earlier(): pl.pallas_call(functools.partial(earlier_kernel, run=run, last=last), in_...  13 us
    all_to_all x1, waiting for transfers between devices, on_device(): lax.all_to_all(queries, axes, split_axis=1, concat_axis=0, tiled=True)  6.42 us
    all_to_all x1, waiting for transfers between devices, on_device(): own = lax.all_to_all(paired, axes, split_axis=1, concat_axis=0, tiled=True)  5.77 us
    all_to_all x1, starting transfers between devices, on_device(): own = lax.all_to_all(paired, axes, split_axis=1, concat_axis=0, tiled=True)  4.74 us
    all_to_all x1, starting transfers between devices, on_device(): lax.all_to_all(queries, axes, split_axis=1, concat_axis=0, tiled=True)  3.49 us
    pallas_call x1, Pallas kernels, attend_own(): pl.pallas_call(functools.partial(own_kernel, run=run), in_specs=[pl.Block...  2.45 us
    ppermute x1, starting transfers between devices, on_device(): far = lax.ppermute(own, 'outer', [(0, 1)])  1.29 us
  transfers between devices with their start and end apart: 5, of which 4 were waited for; matrix products, arithmetic and copies ran while one was open for 1% of the time, Pallas kernels for 14%

profile of v2, /device:TPU:16, one launch (start us, length us, event | category | flops | bytes accessed | tf_op | source)
XLA Modules:
  0.0 63.4 jit_solution(2238730027783317522)
XLA Ops:
  0.0 0.0 copy-start
  0.0 0.9 %copy-done = bf16[64,1024]{1,0:T(8,128)(2,1)S(1)} copy-done((bf16[64,1024]{1,0:T(8,128)(2,1)S(1)}, bf16[64,1024]{1,0:T(8,128)(2,1)}, u32[]{:S(2)}) %copy-start) | copy-done | bytes 131096
  0.9 1.0 %copy_bitcast_fusion.1 = (bf16[64,8,128]{2,0,1:T(8,128)(2,1)S(1)}, bf16[64,8,128]{2,0,1:T(8,128)(2,1)S(1)}) fusion(bf16[64,1024]{1,0:T(8,128)(2,1)S(1)} %copy-done, bf16[64,1024]{1,0:T(8,128)(2,1)} %param.5), kind=kLoop, calls=%fused_computation.2 | loop fusion | bytes 524288 | tf_op jit(solution)/shard_map/reshape | solution.py:169
  1.9 0.0 copy-start.1
  1.9 0.7 %pad_maximum_fusion = bf16[64,8,256]{2,0,1:T(8,128)(2,1)} fusion(bf16[64,8,128]{2,0,1:T(8,128)(2,1)S(1)} %get-tuple-element.19, bf16[64,8,128]{2,0,1:T(8,128)(2,1)S(1)} %get-tuple-element.20), kind=kLoop, calls=%fused_computation.1 | loop fusion | flops 524288 | bytes 524288 | tf_op jit(solution)/shard_map/concatenate | solution.py:168
  2.6 4.7 %all-to-all-start.1 = ((bf16[64,8,256]{2,0,1:T(8,128)(2,1)}), bf16[64,8,256]{2,0,1:T(8,128)(2,1)S(1)}, u32[]{:S(2)}, u32[]{:S(2)}) async-start(bf16[64,8,256]{2,0,1:T(8,128)(2,1)} %pad_maximum_fusion), calls=%async_computation.1 | async-start | bytes 524288 | tf_op jit(solution)/shard_map/all_to_all | solution.py:173
  7.4 0.0 copy-done.1
  7.4 0.8 %copy.15 = bf16[8,8,8,512]{3,2,0,1:T(8,128)(2,1)} copy(bf16[8,8,8,512]{3,2,1,0:T(8,128)(2,1)S(1)} %bitcast.38) | data formatting | bytes 1048576 | tf_op jit(solution)/shard_map/all_to_all | solution.py:174
  8.2 5.8 %all-to-all-done.1 = bf16[64,8,256]{2,0,1:T(8,128)(2,1)S(1)} async-done(((bf16[64,8,256]{2,0,1:T(8,128)(2,1)}), bf16[64,8,256]{2,0,1:T(8,128)(2,1)S(1)}, u32[]{:S(2)}, u32[]{:S(2)}) %all-to-all-start.1) | async-done | bytes 262176 | tf_op jit(solution)/shard_map/all_to_all | solution.py:173
  14.0 3.5 %all-to-all-start = ((bf16[64,8,512]{2,0,1:T(8,128)(2,1)}), bf16[64,8,512]{2,0,1:T(8,128)(2,1)S(1)}, u32[]{:S(2)}, u32[]{:S(2)}) async-start(bf16[64,8,512]{2,0,1:T(8,128)(2,1)} %bitcast.27), calls=%async_computation | async-start | bytes 1048576 | tf_op jit(solution)/shard_map/all_to_all | solution.py:174
  17.5 0.1 collective-permute-start.1
  17.6 1.3 %collective-permute-start = (bf16[512,256]{1,0:T(8,128)(2,1)S(1)}, bf16[512,256]{1,0:T(8,128)(2,1)S(1)}, u32[]{:S(2)}, u32[]{:S(2)}) collective-permute-start(bf16[512,256]{1,0:T(8,128)(2,1)S(1)} %bitcast.35), channel_id=1, source_target_pairs={{0,8},{1,9},{2,10},{3,11},{4,12},{5,13},{6,14},{7,15},{16,24},{17,... | collective-permute-start | bytes 786440 | tf_op jit(solution)/shard_map/ppermute | solution.py:176
  18.9 0.2 collective-permute-done.1.other_ref
  19.1 6.4 %all-to-all-done = bf16[64,8,512]{2,0,1:T(8,128)(2,1)S(1)} async-done(((bf16[64,8,512]{2,0,1:T(8,128)(2,1)}), bf16[64,8,512]{2,0,1:T(8,128)(2,1)S(1)}, u32[]{:S(2)}, u32[]{:S(2)}) %all-to-all-start) | async-done | bytes 524320 | tf_op jit(solution)/shard_map/all_to_all | solution.py:174
  25.5 2.5 %attend_own.1 = (f32[2048,128]{1,0:T(8,128)S(1)}, f32[2048,128]{1,0:T(8,128)S(1)}) custom-call(s32[1]{0:T(128)} %bitcast.5.core_ref, bf16[512,512]{1,0:T(8,128)(2,1)S(1)} %bitcast.28, bf16[512,256]{1,0:T(8,128)(2,1)S(1)} %bitcast.36, bf16[512,256]{1,0:T(8,128)(2,1)S(1)} %collective-permute-done.1.other_ref), custom_call_target="tpu_custom_call" | custom-call | flops 1073741824 | bytes 1048576 | tf_op jit(solution)/shard_map/attend_own/pallas_call | solution.py:128
  28.0 1.2 %collective-permute-done = bf16[512,256]{1,0:T(8,128)(2,1)S(1)} collective-permute-done((bf16[512,256]{1,0:T(8,128)(2,1)S(1)}, bf16[512,256]{1,0:T(8,128)(2,1)S(1)}, u32[]{:S(2)}, u32[]{:S(2)}) %collective-permute-start) | collective-permute-done | bytes 262176 | tf_op jit(solution)/shard_map/ppermute | solution.py:176
  29.2 0.0 collective-permute-start.2
  29.2 6.4 %attend_earlier.1 = (f32[2048,128]{1,0:T(8,128)S(1)}, f32[2048,128]{1,0:T(8,128)S(1)}) custom-call(s32[1]{0:T(128)} %bitcast.count_ref, bf16[512,512]{1,0:T(8,128)(2,1)S(1)} %bitcast.29, bf16[1,512,256]{2,1,0:T(8,128)(2,1)S(1)} %bitcast.32, f32[2048,128]{1,0:T(8,128)S(1)} %get-tuple-element.15.summed_in, f32[2048,128]{1,0:T(8,128)S(1)} %get-tuple-element.16.state_in), custom_call_target="tpu_custom_call" | custom-call | flops 536870912 | bytes 1048576 | tf_op jit(solution)/shard_map/attend_earlier/pallas_call | solution.py:150
  35.5 0.0 collective-permute-done.2
  35.5 6.6 %attend_last.1 = bf16[512,512]{1,0:T(8,128)(2,1)S(1)} custom-call(s32[1]{0:T(128)} %bitcast.count_ref, bf16[512,512]{1,0:T(8,128)(2,1)S(1)} %bitcast.30, bf16[1,512,256]{2,1,0:T(8,128)(2,1)S(1)} %bitcast.33, f32[2048,128]{1,0:T(8,128)S(1)} %get-tuple-element.17.summed_in, f32[2048,128]{1,0:T(8,128)S(1)} %get-tuple-element.18.state_in), custom_call_target="tpu_custom_call" | custom-call | flops 536870912 | bytes 1048576 | tf_op jit(solution)/shard_map/attend_last/pallas_call | solution.py:150
  42.2 20.3 %all_to_all.54 = bf16[8,64,512]{2,1,0:T(8,128)(2,1)S(1)} all-to-all(bf16[8,64,512]{2,1,0:T(8,128)(2,1)S(1)} %bitcast.31), channel_id=1, replica_groups=mesh['head'=2,'outer'=2,'inner'=4,'core'=2] {'inner','head'}, dimensions={0} | all-to-all | bytes 1048576 | tf_op jit(solution)/shard_map/all_to_all | solution.py:188
  62.5 0.8 %copy.11 = bf16[8,8,8,512]{3,2,0,1:T(8,128)(2,1)} copy(bf16[8,8,8,512]{3,2,1,0:T(8,128)(2,1)S(1)} %bitcast.37) | data formatting | bytes 1048576 | tf_op jit(solution)/shard_map/all_to_all | solution.py:188
Async XLA Ops:
  0.0 0.9 %copy-start = (bf16[64,1024]{1,0:T(8,128)(2,1)S(1)}, bf16[64,1024]{1,0:T(8,128)(2,1)}, u32[]{:S(2)}) copy-start(bf16[64,1024]{1,0:T(8,128)(2,1)} %param.4) | copy-start | bytes 393220
  1.9 5.5 %copy-start.1 = (bf16[64,4096]{1,0:T(8,128)(2,1)S(1)}, bf16[64,4096]{1,0:T(8,128)(2,1)}, u32[]{:S(2)}) copy-start(bf16[64,4096]{1,0:T(8,128)(2,1)} %param.3) | copy-start | bytes 1572868
  2.6 11.4 %all-to-all-start.1 = ((bf16[64,8,256]{2,0,1:T(8,128)(2,1)}), bf16[64,8,256]{2,0,1:T(8,128)(2,1)S(1)}, u32[]{:S(2)}, u32[]{:S(2)}) async-start(bf16[64,8,256]{2,0,1:T(8,128)(2,1)} %pad_maximum_fusion), calls=%async_computation.1 | async-start | bytes 524288 | tf_op jit(solution)/shard_map/all_to_all | solution.py:173
  14.0 11.5 %all-to-all-start = ((bf16[64,8,512]{2,0,1:T(8,128)(2,1)}), bf16[64,8,512]{2,0,1:T(8,128)(2,1)S(1)}, u32[]{:S(2)}, u32[]{:S(2)}) async-start(bf16[64,8,512]{2,0,1:T(8,128)(2,1)} %bitcast.27), calls=%async_computation | async-start | bytes 1048576 | tf_op jit(solution)/shard_map/all_to_all | solution.py:174
  17.5 1.6 %collective-permute-start.1 = (bf16[512,256]{1,0:T(8,128)(2,1)S(1)}, bf16[512,256]{1,0:T(8,128)(2,1)S(1)}, u32[]{:S(2)}, u32[]{:S(2)}) collective-permute-start(bf16[512,256]{1,0:T(8,128)(2,1)S(1)} %bitcast.34), channel_id=1, source_target_pairs={{0,1},{1,0},{2,3},{3,2},{4,5},{5,4},{6,7},{7,6},{8,9},{9,8},{10,11... | collective-permute-start | bytes 786440 | tf_op jit(solution)/shard_map/ppermute | solution.py:177
  17.6 11.6 %collective-permute-start = (bf16[512,256]{1,0:T(8,128)(2,1)S(1)}, bf16[512,256]{1,0:T(8,128)(2,1)S(1)}, u32[]{:S(2)}, u32[]{:S(2)}) collective-permute-start(bf16[512,256]{1,0:T(8,128)(2,1)S(1)} %bitcast.35), channel_id=1, source_target_pairs={{0,8},{1,9},{2,10},{3,11},{4,12},{5,13},{6,14},{7,15},{16,24},{17,... | collective-permute-start | bytes 786440 | tf_op jit(solution)/shard_map/ppermute | solution.py:176
  29.2 6.4 %collective-permute-start.2 = (bf16[512,256]{1,0:T(8,128)(2,1)S(1)}, bf16[512,256]{1,0:T(8,128)(2,1)S(1)}, u32[]{:S(2)}, u32[]{:S(2)}) collective-permute-start(bf16[512,256]{1,0:T(8,128)(2,1)S(1)} %collective-permute-done), channel_id=1, source_target_pairs={{0,1},{1,0},{2,3},{3,2},{4,5},{5,4},{6,7},{7,6},{8,9},{9,8},{10,11... | collective-permute-start | bytes 786440 | tf_op jit(solution)/shard_map/ppermute | solution.py:180
